TPU v7x, 32 devices: a whole 2x2x4 slice. The times are simulated.
32 devices in a mesh: mem: 8 (over z, x), rep: 4 (over y, core).
Axes of the slice: x: 2, y: 2, z: 4, core: 2. Of those that a mesh axis runs over, the one named last changes fastest.
Arguments:
- memory: float32 [8192, 172], P('mem'), may hold values from -6 to 6
- node_slot: int32 [8192], replicated, may hold values from 0 to 8191, as said below
- event_nodes: int32 [2, 4096, 33], P(None, ('mem', 'rep')), may hold values from 0 to 8191, as said below
- event_times: int32 [2, 4096], P(None, ('mem', 'rep')), may hold values from 0 to 999
- valid_mask: int32 [2, 4096], P(None, ('mem', 'rep')), may hold values 0 or 1
- time_freq: float32 [100], replicated, may hold values from 0.001 to 1
- time_phase: float32 [100], replicated, may hold values from -3.140625 to 3.140625
- gru_input: bfloat16 [444, 516], replicated, may hold values from -0.25 to 0.25
- gru_hidden: bfloat16 [172, 516], replicated, may hold values from -0.4375 to 0.4375
- gru_in_bias: float32 [516], replicated, may hold values from -3 to 3
- gru_hid_bias: float32 [516], replicated, may hold values from -3 to 3
- w_self: float32 [172, 100], replicated, may hold values from -0.4375 to 0.4375
- w_nbr: float32 [172, 100], replicated, may hold values from -0.4375 to 0.4375
- b_embed: float32 [100], replicated, may hold values from -3 to 3
- w_dec1: float32 [200, 100], replicated, may hold values from -0.4375 to 0.4375
- b_dec1: float32 [100], replicated, may hold values from -3 to 3
- w_dec2: float32 [100], replicated, may hold values from -0.625 to 0.625
- b_dec2: float32 [1], replicated, may hold values from -3 to 3
Outputs:
- memory_out: float32 [8192, 172], P('mem')
- batch_losses: float32 [2], replicated
- w_self_out: float32 [172, 100], replicated
- w_nbr_out: float32 [172, 100], replicated
- b_embed_out: float32 [100], replicated
- w_dec1_out: float32 [200, 100], replicated
- b_dec1_out: float32 [100], replicated
- w_dec2_out: float32 [100], replicated
- b_dec2_out: float32 [1], replicated
Inputs may be any that keep to these rules, and one draw needn't show every extreme that they name: A permutation: node n's memory is row node_slot[n] of memory. `event_nodes`: columns 0, 1, 2 of an event are its source, destination and negative node; column 3 + r * 10 + k is neighbour k of column r. Among one device's events of one batch, the nodes of columns 0 and 1 whose slots lie in one block of 1024 slots are at most 64, and those of the other columns at most 620; in every such group of events one block of slots receives exactly 64 and 620.
All inputs are finite; a program needn't handle non-finite values. No bound on the sum of `valid_mask` on one device may be relied on, other than what follows from the above.
Results may differ from a plain program's by a relative error of at most 0.002.
Values may be sent and summed in bfloat16 or wider, within the bound.
A program may use at most 128 MiB of HBM per device.

v0:
```python
import jax
import jax.numpy as jnp
from jax import lax
from jax.sharding import PartitionSpec as P

step_size = 4.0


def block_loss(current, own_rows, beside_sum, neighbours, valid_part):
    w_self, w_nbr, b_embed, w_dec1, b_dec1, w_dec2, b_dec2 = current
    num_events = own_rows.shape[0] // 3
    direct = jnp.dot(own_rows, w_self.astype(jnp.bfloat16), preferred_element_type=jnp.float32)
    spread = jnp.dot(
        beside_sum, w_nbr.astype(jnp.bfloat16).astype(jnp.float32), precision=lax.Precision.HIGHEST
    )
    hidden = jnp.tanh(direct + spread * (1.0 / neighbours) + b_embed).astype(jnp.bfloat16)
    first = hidden[:num_events]
    paired = jnp.concatenate([jnp.concatenate([first, first], 0), hidden[num_events:]], 1)
    inner_act = jax.nn.relu(
        jnp.dot(paired, w_dec1.astype(jnp.bfloat16), preferred_element_type=jnp.float32) + b_dec1
    )
    logits = jnp.sum(inner_act * w_dec2, 1) + b_dec2[0]
    weights = valid_part.astype(jnp.float32)
    sign_flip = jnp.concatenate(
        [-jnp.ones((num_events,), jnp.float32), jnp.ones((num_events,), jnp.float32)]
    )
    return jnp.sum(jax.nn.softplus(sign_flip * logits) * jnp.concatenate([weights, weights]))


def normalized_step(params, gradients):
    total = jnp.zeros((), jnp.float32)
    for grad_part in gradients:
        total = total + jnp.sum(grad_part * grad_part)
    factor = step_size / (jnp.sqrt(total) + 1e-06)
    return tuple((value - factor * grad_part for value, grad_part in zip(params, gradients)))


def memory_update(mean_rest, state_bf, old_state, gru_input, gru_hidden, gru_in_bias, gru_hid_bias):
    row_width = old_state.shape[1]
    from_input = (
        jnp.dot(state_bf, gru_input[:row_width], preferred_element_type=jnp.float32)
        + jnp.dot(mean_rest, gru_input[row_width:], preferred_element_type=jnp.float32)
        + gru_in_bias
    )
    from_state = jnp.dot(state_bf, gru_hidden, preferred_element_type=jnp.float32) + gru_hid_bias
    reset = jax.nn.sigmoid(from_input[:, :row_width] + from_state[:, :row_width])
    update = jax.nn.sigmoid(
        from_input[:, row_width : 2 * row_width] + from_state[:, row_width : 2 * row_width]
    )
    candidate = jnp.tanh(from_input[:, 2 * row_width :] + reset * from_state[:, 2 * row_width :])
    return (1.0 - update) * candidate + update * old_state


def look_up(table, ids):
    width = 128
    groups = table.shape[0] // width
    grid = table.reshape(groups, width)
    digits = jnp.concatenate([grid >> 8, grid & 255], 1).astype(jnp.bfloat16)
    pick = ((ids // width)[..., None] == jnp.arange(groups, dtype=jnp.int32)).astype(jnp.bfloat16)
    rows = jnp.dot(pick, digits, preferred_element_type=jnp.float32)
    here = (ids % width)[..., None] == jnp.arange(width, dtype=jnp.int32)
    both = jnp.where(here, rows[..., :width] * 256.0 + rows[..., width:], 0.0)
    return jnp.sum(both, -1).astype(jnp.int32)


def sum_everywhere(gradients, loss_local, count_local, devices):
    g_self, g_nbr, g_embed, g_dec1, g_bias1, g_dec2, g_bias2 = gradients
    width = g_self.shape[1]
    scalars = jnp.concatenate([g_bias2, loss_local[None], count_local[None]])
    scalars = jnp.pad(scalars, (0, width - scalars.shape[0]))
    table = jnp.concatenate(
        [g_self, g_nbr, g_dec1, jnp.stack([g_embed, g_bias1, g_dec2, scalars])], 0
    )
    used = table.shape[0]
    share = -(-used // (devices * 8)) * 8
    table = jnp.pad(table, ((0, share * devices - used), (0, 0))).reshape(devices, share, width)
    parts = lax.all_to_all(table, ("mem", "rep"), split_axis=0, concat_axis=0, tiled=True)
    total = lax.all_gather(jnp.sum(parts, 0), ("mem", "rep"), axis=0, tiled=True)
    n_self, n_nbr, n_dec1 = (g_self.shape[0], g_nbr.shape[0], g_dec1.shape[0])
    at = n_self + n_nbr + n_dec1
    return (
        (
            total[:n_self],
            total[n_self : n_self + n_nbr],
            total[at],
            total[n_self + n_nbr : at],
            total[at + 1],
            total[at + 2],
            total[at + 3, :1],
        ),
        total[at + 3, 1],
        total[at + 3, 2],
    )


def place_rows(owner_ids, owners, stride, offset):
    length = owner_ids.shape[0]
    width = 128
    groups = -(-length // width)
    padded_ids = owner_ids.reshape(groups, width)
    one_hot = (padded_ids[:, :, None] == jnp.arange(owners, dtype=jnp.int32)[None, None, :]).astype(
        jnp.float32
    )
    lower = (
        jnp.arange(width, dtype=jnp.int32)[:, None] > jnp.arange(width, dtype=jnp.int32)[None, :]
    ).astype(jnp.float32)
    within = jnp.einsum("ij,gjo->gio", lower, one_hot, precision=lax.Precision.HIGHEST)
    totals = jnp.sum(one_hot, 1)
    starts = jnp.cumsum(totals, 0) - totals
    before = jnp.sum((within + starts[:, None, :]) * one_hot, 2).reshape(-1)
    return owner_ids * stride + offset + before.astype(jnp.int32)


def body(
    memory,
    node_slot,
    event_nodes,
    event_times,
    valid_mask,
    time_freq,
    time_phase,
    gru_input,
    gru_hidden,
    gru_in_bias,
    gru_hid_bias,
    w_self,
    w_nbr,
    b_embed,
    w_dec1,
    b_dec1,
    w_dec2,
    b_dec2,
):
    owners = lax.axis_size("mem")
    devices = owners * lax.axis_size("rep")
    node_dev, row_width = memory.shape
    batches, events, columns = event_nodes.shape
    neighbours = (columns - 3) // 3
    cap_pair = 2 * events // owners * 2
    params = (w_self, w_nbr, b_embed, w_dec1, b_dec1, w_dec2, b_dec2)
    losses = []
    all_slots = look_up(node_slot, event_nodes.transpose(0, 2, 1))
    for batch_index in range(batches):
        slot_ids = all_slots[batch_index]
        memory_bf = memory.astype(jnp.bfloat16)
        whole_bf = lax.all_gather(memory_bf, "mem", axis=0, tiled=True)
        fetched = jnp.take(whole_bf, slot_ids.reshape(-1), axis=0, mode="clip")
        own_rows = fetched[: 3 * events]
        beside = fetched[3 * events :].reshape(3, neighbours, events, row_width)
        beside_sum = jnp.sum(beside.astype(jnp.float32), 1).reshape(3 * events, row_width)
        pair_slots = slot_ids[:2].reshape(-1)
        pair_at = place_rows(pair_slots // node_dev, owners, cap_pair, 0)
        offsets = (pair_slots % node_dev).astype(jnp.int32)
        time_code = jnp.cos(
            event_times[batch_index].astype(jnp.float32)[:, None] * time_freq + time_phase
        ).astype(jnp.bfloat16)
        marks = jnp.stack([jnp.ones_like(offsets), offsets // 128, offsets % 128], 1)
        partners = jnp.concatenate([own_rows[events : 2 * events], own_rows[:events]], 0)
        letters = jnp.concatenate(
            [partners, jnp.concatenate([time_code, time_code], 0), marks.astype(jnp.bfloat16)], 1
        )
        seats = jnp.arange(owners * cap_pair, dtype=jnp.int32)[:, None] == pair_at[None, :]
        parcel = jnp.dot(
            seats.astype(jnp.bfloat16), letters, preferred_element_type=jnp.float32
        ).astype(jnp.bfloat16)
        parcel = parcel.reshape(owners, cap_pair, letters.shape[1])
        parcel = lax.all_to_all(parcel, "mem", split_axis=0, concat_axis=0, tiled=True)
        every_parcel = lax.all_gather(parcel, "rep", axis=0, tiled=True)
        every_parcel = every_parcel.reshape(-1, letters.shape[1])
        digits = every_parcel[:, -2:].astype(jnp.int32)
        target = digits[:, 0] * 128 + digits[:, 1]
        matches = jnp.arange(node_dev, dtype=jnp.int32)[:, None] == target[None, :]
        summed = jnp.dot(
            matches.astype(jnp.bfloat16), every_parcel, preferred_element_type=jnp.float32
        )
        counts = summed[:, -3:-2]
        mean_rest = (summed[:, :-3] / jnp.maximum(counts, 1.0)).astype(jnp.bfloat16)
        fresh = memory_update(
            mean_rest, memory_bf, memory, gru_input, gru_hidden, gru_in_bias, gru_hid_bias
        )
        memory = jnp.where(counts > 0, fresh, memory)
        valid_part = valid_mask[batch_index]
        loss_local, pullback = jax.vjp(
            lambda current: block_loss(current, own_rows, beside_sum, neighbours, valid_part),
            params,
        )
        gradients = pullback(jnp.ones_like(loss_local))[0]
        count_local = jnp.sum(valid_part.astype(jnp.float32))
        gradients, loss_total, count_total = sum_everywhere(
            gradients, loss_local, count_local, devices
        )
        params = normalized_step(params, gradients)
        losses.append(loss_total / jnp.maximum(count_total, 1.0))
    return (
        memory,
        jnp.stack(losses),
        params[0],
        params[1],
        params[2],
        params[3],
        params[4],
        params[5],
        params[6],
    )


def solution(mesh):
    return jax.shard_map(
        body,
        mesh=mesh,
        in_specs=(
            P("mem", None),
            P(),
            P(None, ("mem", "rep"), None),
            P(None, ("mem", "rep")),
            P(None, ("mem", "rep")),
            P(),
            P(),
            P(),
            P(),
            P(),
            P(),
            P(),
            P(),
            P(),
            P(),
            P(),
            P(),
            P(),
        ),
        out_specs=(P("mem", None), P(), P(), P(), P(), P(), P(), P(), P()),
        check_vma=False,
    )
```

profile of v0, /device:TPU:0, one launch (start us, length us, event | category | flops | bytes accessed | tf_op | source)
XLA Modules:
  0.0 355.3 jit_solution(9725286313087995322)
XLA Ops:
  7.2 2.2 copy.57
  12.5 3.1 fusion.3
  18.3 67.9 %all-gather.5.cloned.1.call-done = bf16[8192,172]{1,0:T(8,128)(2,1)} async-done(((bf16[1024,172]{1,0:T(8,128)(2,1)}), bf16[8192,172]{1,0:T(8,128)(2,1)}) %all-gather.5.cloned.1.call-update) | async-done | bytes 2818064 | tf_op jit(solution)/shard_map/all_gather | solution.py:146
  86.3 12.3 %gather_fusion = bf16[4224,172]{1,0:T(8,128)(2,1)S(1)} fusion(bf16[8192,172]{1,0:T(8,128)(2,1)} %all-gather.5.cloned.1.call-done, s32[5120]{0:T(1024)S(1)} %pad_clamp_fusion.1), kind=kCustom, calls=%fused_computation | custom fusion | bytes 2923008 | tf_op jit(solution)/shard_map/jit(_take)/gather | solution.py:147
  102.0 15.1 %all_to_all.20 = bf16[8,64,275]{2,1,0:T(8,128)(2,1)} all-to-all(bf16[8,64,275]{2,1,0:T(8,128)(2,1)S(1)} %bitcast.175), channel_id=1, replica_groups=mesh['mem'=8,'rep'=4] {'mem'}, dimensions={0} | all-to-all | bytes 563200 | tf_op jit(solution)/shard_map/all_to_all | solution.py:167
  117.4 1.8 convolution_add_fusion
  119.2 1.8 fusion.66
  121.0 14.4 %all-gather.7.cloned.1.call-done = bf16[32,64,275]{2,1,0:T(8,128)(2,1)} async-done(((bf16[8,64,275]{2,1,0:T(8,128)(2,1)}), bf16[32,64,275]{2,1,0:T(8,128)(2,1)}) %all-gather.7.cloned.1.call-update) | async-done | bytes 1126416 | tf_op jit(solution)/shard_map/all_gather | solution.py:168
  137.6 2.0 fusion.1
  147.8 2.0 fusion.127
  152.3 4.6 %all-to-all-start.2 = ((f32[32,24,100]{2,1,0:T(8,128)}), f32[32,24,100]{2,1,0:T(8,128)S(1)}, u32[]{:S(2)}, u32[]{:S(2)}) async-start(f32[32,24,100]{2,1,0:T(8,128)} %bitcast.37), calls=%async_computation.2 | async-start | bytes 786432 | tf_op jit(solution)/shard_map/all_to_all | solution.py:77
  157.9 18.0 %all-to-all-done.2 = f32[32,24,100]{2,1,0:T(8,128)S(1)} async-done(((f32[32,24,100]{2,1,0:T(8,128)}), f32[32,24,100]{2,1,0:T(8,128)S(1)}, u32[]{:S(2)}, u32[]{:S(2)}) %all-to-all-start.2) | async-done | bytes 307232 | tf_op jit(solution)/shard_map/all_to_all | solution.py:77
  175.9 42.3 %all_gather.22 = f32[768,100]{1,0:T(8,128)S(1)} all-gather(f32[24,100]{1,0:T(8,128)S(1)} %reduce_sum.364), channel_id=1, replica_groups=mesh['mem'=8,'rep'=4] {'mem','rep'}, dimensions={0}, use_global_device_ids=true | all-gather | bytes 316800 | tf_op jit(solution)/shard_map/all_gather | solution.py:78
  226.7 5.8 %copy.62 = bf16[8192,172]{1,0:T(8,128)(2,1)} copy(bf16[8192,172]{0,1:T(8,128)(2,1)} %all-gather.9.cloned.1.call-done) | data formatting | bytes 5636096 | tf_op jit(solution)/shard_map/all_gather | solution.py:146
  232.5 12.3 %gather_fusion.1 = bf16[4224,172]{1,0:T(8,128)(2,1)S(1)} fusion(bf16[8192,172]{1,0:T(8,128)(2,1)} %copy.62, s32[5120]{0:T(1024)S(1)} %pad_clamp_fusion), kind=kCustom, calls=%fused_computation.1 | custom fusion | bytes 2923008 | tf_op jit(solution)/shard_map/jit(_take)/gather | solution.py:147
  254.6 4.2 %all-to-all-start.1 = ((bf16[8,64,275]{2,1,0:T(8,128)(2,1)}), bf16[8,64,275]{2,1,0:T(8,128)(2,1)}, u32[]{:S(2)}, u32[]{:S(2)}) async-start(bf16[8,64,275]{2,1,0:T(8,128)(2,1)} %bitcast.174), calls=%async_computation.1 | async-start | bytes 786432 | tf_op jit(solution)/shard_map/all_to_all | solution.py:167
  259.9 2.0 fusion.126
  261.9 1.8 fusion.15
  265.5 2.0 concatenate.86
  268.3 3.0 all-to-all-done.1
  271.3 2.7 all-to-all-start.3
  277.6 9.7 %all-to-all-done.3 = f32[32,24,100]{2,1,0:T(8,128)S(1)} async-done(((f32[32,24,100]{2,1,0:T(8,128)}), f32[32,24,100]{2,1,0:T(8,128)S(1)}, u32[]{:S(2)}, u32[]{:S(2)}) %all-to-all-start.3) | async-done | bytes 307232 | tf_op jit(solution)/shard_map/all_to_all | solution.py:77
  287.3 39.6 %all_gather.23 = f32[768,100]{1,0:T(8,128)S(1)} all-gather(f32[24,100]{1,0:T(8,128)S(1)} %reduce_sum.380), channel_id=1, replica_groups=mesh['mem'=8,'rep'=4] {'mem','rep'}, dimensions={0}, use_global_device_ids=true | all-gather | bytes 316800 | tf_op jit(solution)/shard_map/all_gather | solution.py:78
  343.0 2.0 fusion
  (191 shorter events, 51.8 us)
Async XLA Ops:
  7.2 110.2 %copy-start = (bf16[172,516]{1,0:T(8,128)(2,1)S(1)}, bf16[172,516]{1,0:T(8,128)(2,1)}, u32[]{:S(2)}) copy-start(bf16[172,516]{1,0:T(8,128)(2,1)} %param.27) | copy-start | bytes 532516
  7.2 79.1 %all-gather.5.cloned.1.call-start = ((), (), s32[]{:S(2)}) async-start(), calls=%async_computation.4 | async-start | bytes 4718592 | tf_op jit(solution)/shard_map/all_gather | solution.py:146
  9.4 126.0 %all-gather.7.cloned.1.call-start = ((), (), s32[]{:S(2)}) async-start(), calls=%async_computation.5 | async-start | bytes 1966080 | tf_op jit(solution)/shard_map/all_gather | solution.py:168
  12.5 3.9 %copy-start.33 = (s32[2,128]{1,0:T(2,128)S(1)}, s32[2,128]{1,0:T(2,128)}, u32[]{:S(2)}) copy-start(s32[2,128]{1,0:T(2,128)} %param.22) | copy-start | bytes 3076
  12.5 3.9 %copy-start.34 = (f32[100]{0:T(128)S(1)}, f32[100]{0:T(128)}, u32[]{:S(2)}) copy-start(f32[100]{0:T(128)} %param.25) | copy-start | bytes 1204
  12.5 3.9 %copy-start.35 = (f32[100]{0:T(128)S(1)}, f32[100]{0:T(128)}, u32[]{:S(2)}) copy-start(f32[100]{0:T(128)} %param.24) | copy-start | bytes 1204
  98.6 18.8 %copy-start.2 = (bf16[1024,172]{1,0:T(8,128)(2,1)S(1)}, bf16[1024,172]{1,0:T(8,128)(2,1)}, u32[]{:S(2)}) copy-start(bf16[1024,172]{1,0:T(8,128)(2,1)} %copy.57) | copy-start | bytes 1056772
  98.6 18.8 %copy-start.17 = (f32[516]{0:T(1024)S(1)}, f32[516]{0:T(1024)}, u32[]{:S(2)}) copy-start(f32[516]{0:T(1024)} %param.29) | copy-start | bytes 6196
  117.1 109.6 %all-gather.9.cloned.1.call-start = ((), (), s32[]{:S(2)}) async-start(), calls=%async_computation.6 | async-start | bytes 3244032 | tf_op jit(solution)/shard_map/all_gather | solution.py:146
  152.3 23.5 %all-to-all-start.2 = ((f32[32,24,100]{2,1,0:T(8,128)}), f32[32,24,100]{2,1,0:T(8,128)S(1)}, u32[]{:S(2)}, u32[]{:S(2)}) async-start(f32[32,24,100]{2,1,0:T(8,128)} %bitcast.37), calls=%async_computation.2 | async-start | bytes 786432 | tf_op jit(solution)/shard_map/all_to_all | solution.py:77
  226.6 19.0 %copy-start.22 = (f32[100]{0:T(128)}, f32[100]{0:T(128)S(1)}, u32[]{:S(2)}) copy-start(f32[100]{0:T(128)S(1)} %get-tuple-element.57) | copy-start | bytes 1204
  226.6 20.0 %copy-start.28 = (f32[100]{0:T(128)}, f32[100]{0:T(128)S(1)}, u32[]{:S(2)}) copy-start(f32[100]{0:T(128)S(1)} %get-tuple-element.58) | copy-start | bytes 1204
  226.6 23.1 %copy-start.20 = (f32[100]{0:T(128)}, f32[100]{0:T(128)S(1)}, u32[]{:S(2)}) copy-start(f32[100]{0:T(128)S(1)} %get-tuple-element.56) | copy-start | bytes 1204
  250.7 14.8 %copy-start.31 = (f32[100]{0:T(128)S(1)}, f32[100]{0:T(128)}, u32[]{:S(2)}) copy-start(f32[100]{0:T(128)} %get-tuple-element.29) | copy-start | bytes 1204
  250.7 14.8 %copy-start.32 = (f32[100]{0:T(128)S(1)}, f32[100]{0:T(128)}, u32[]{:S(2)}) copy-start(f32[100]{0:T(128)} %get-tuple-element.30) | copy-start | bytes 1204
  254.6 20.6 %copy-start.3 = (bf16[1024,172]{0,1:T(8,128)(2,1)S(1)}, bf16[1024,172]{0,1:T(8,128)(2,1)}, u32[]{:S(2)}) copy-start(bf16[1024,172]{0,1:T(8,128)(2,1)} %get-tuple-element.39) | copy-start | bytes 1056772
  254.6 16.7 %all-to-all-start.1 = ((bf16[8,64,275]{2,1,0:T(8,128)(2,1)}), bf16[8,64,275]{2,1,0:T(8,128)(2,1)}, u32[]{:S(2)}, u32[]{:S(2)}) async-start(bf16[8,64,275]{2,1,0:T(8,128)(2,1)} %bitcast.174), calls=%async_computation.1 | async-start | bytes 786432 | tf_op jit(solution)/shard_map/all_to_all | solution.py:167
  263.7 11.5 %copy-start.13 = (bf16[444,516]{0,1:T(8,128)(2,1)S(1)}, bf16[444,516]{0,1:T(8,128)(2,1)}, u32[]{:S(2)}) copy-start(bf16[444,516]{0,1:T(8,128)(2,1)} %param.26) | copy-start | bytes 1374628
  268.3 8.8 %copy-start.18 = (f32[516]{0:T(1024)S(1)}, f32[516]{0:T(1024)}, u32[]{:S(2)}) copy-start(f32[516]{0:T(1024)} %param.29) | copy-start | bytes 6196
  271.3 16.0 %all-to-all-start.3 = ((f32[32,24,100]{2,1,0:T(8,128)}), f32[32,24,100]{2,1,0:T(8,128)S(1)}, u32[]{:S(2)}, u32[]{:S(2)}) async-start(f32[32,24,100]{2,1,0:T(8,128)} %bitcast.56), calls=%async_computation.3 | async-start | bytes 786432 | tf_op jit(solution)/shard_map/all_to_all | solution.py:77
  274.0 66.9 %all-gather.11.cloned.1.call-start = ((), (), s32[]{:S(2)}) async-start(), calls=%async_computation.7 | async-start | bytes 1966080 | tf_op jit(solution)/shard_map/all_gather | solution.py:168
  277.0 60.2 %copy-start.21 = (f32[100]{0:T(128)S(1)}, f32[100]{0:T(128)}, u32[]{:S(2)}) copy-start(f32[100]{0:T(128)} %copy-done.20) | copy-start | bytes 1204
  277.0 60.2 %copy-start.23 = (f32[100]{0:T(128)S(1)}, f32[100]{0:T(128)}, u32[]{:S(2)}) copy-start(f32[100]{0:T(128)} %copy-done.22) | copy-start | bytes 1204
  277.0 60.2 %copy-start.29 = (f32[100]{0:T(128)S(1)}, f32[100]{0:T(128)}, u32[]{:S(2)}) copy-start(f32[100]{0:T(128)} %copy-done.28) | copy-start | bytes 1204
  (22 other events, 37.8 us)
Sparse Core Ops, SparseCore 0:
  10.7 75.5 all-gather.4
  117.2 18.1 all-gather.6
  143.1 65.9 all-gather.8
  277.2 21.7 all-gather.10
where the time goes:
time: 357 us; the launch traced here: 355 us
  waiting for transfers between devices  113 us (32%)
  blocking collectives  97 us (27%)
  local copies, waits for them, and re-layouts  45.8 us (13%)
  other arithmetic  32.9 us (9%)
  between operations  30.8 us (9%)
  matrix products  23.9 us (7%)
  starting transfers between devices  11.9 us (3%)
    all_gather x2, blocking collectives, sum_everywhere(): lax.all_gather(jnp.sum(parts, 0), ('mem', 'rep'), axis=0, tiled=True)  81.9 us
    all_gather x2, waiting for transfers between devices, body(): whole_bf = lax.all_gather(memory_bf, 'mem', axis=0, tiled=True)  67.9 us
    all_to_all x2, waiting for transfers between devices, sum_everywhere(): lax.all_to_all(table, ('mem', 'rep'), split_axis=0, concat_axis=0, tiled=...  27.7 us
    gather x2, local copies, waits for them, and re-layouts, body(): fetched = jnp.take(whole_bf, slot_ids.reshape(-1), axis=0, mode='clip')  24.7 us
    all_to_all x1, blocking collectives, body(): lax.all_to_all(parcel, 'mem', split_axis=0, concat_axis=0, tiled=True)  15.1 us
    all_gather x2, waiting for transfers between devices, body(): every_parcel = lax.all_gather(parcel, 'rep', axis=0, tiled=True)  14.4 us
    all_to_all x2, starting transfers between devices, sum_everywhere(): lax.all_to_all(table, ('mem', 'rep'), split_axis=0, concat_axis=0, tiled=...  7.3 us
  transfers between devices with their start and end apart: 7, of which 5 were waited for; matrix products, arithmetic and copies ran while one was open for 12% of the time, Pallas kernels for 0%

commit v1 on v0

--- a/solution.py
+++ b/solution.py
@@ -143,7 +143,14 @@
     for batch_index in range(batches):
         slot_ids = all_slots[batch_index]
         memory_bf = memory.astype(jnp.bfloat16)
-        whole_bf = lax.all_gather(memory_bf, "mem", axis=0, tiled=True)
+        ring = [memory_bf]
+        for hop in range(7):
+            ring.append(lax.ppermute(ring[-1], "mem", [(dev, (dev + 1) % 8) for dev in range(8)]))
+        whole_bf = jnp.roll(
+            jnp.concatenate(ring[::-1], axis=0),
+            (lax.axis_index("mem") + 1) * ring[0].shape[0],
+            axis=0,
+        )
         fetched = jnp.take(whole_bf, slot_ids.reshape(-1), axis=0, mode="clip")
         own_rows = fetched[: 3 * events]
         beside = fetched[3 * events :].reshape(3, neighbours, events, row_width)

time: 357 us -> 440 us (1.23)
  waiting for transfers between devices: 113 us -> 166 us
  other arithmetic: 32.9 us -> 54.4 us
  blocking collectives: 97 us -> 82.6 us
  starting transfers between devices: 11.9 us -> 23.8 us
  local copies, waits for them, and re-layouts: 45.8 us -> 53.6 us
    ppermute x0 -> x14, waiting for transfers between devices: none -> 138 us  [body(): lax.ppermute(ring[-1], 'mem', [(dev, (dev + 1) % 8) for dev in range(8)])]
    all_gather x2 -> x0, waiting for transfers between devices: 67.9 us -> none  [body(): whole_bf = lax.all_gather(memory_bf, 'mem', axis=0, tiled=True)]
    all_to_all x2, waiting for transfers between devices: 27.7 us -> 9.99 us  [sum_everywhere(): lax.all_to_all(table, ('mem', 'rep'), split_axis=0, concat_axis=0, tiled=...]
    all_to_all x1 -> x0, blocking collectives: 15.1 us -> none  [body(): lax.all_to_all(parcel, 'mem', split_axis=0, concat_axis=0, tiled=True)]
    concatenate x0 -> x2, other arithmetic: none -> 14.9 us  [body(): jnp.roll(jnp.concatenate(ring[::-1], axis=0), (lax.axis_index('mem') + 1)...]
    all_gather x1 -> x0, local copies, waits for them, and re-layouts: 5.81 us -> none  [body(): whole_bf = lax.all_gather(memory_bf, 'mem', axis=0, tiled=True)]
    ppermute x0 -> x14, starting transfers between devices: none -> 5.11 us  [body(): lax.ppermute(ring[-1], 'mem', [(dev, (dev + 1) % 8) for dev in range(8)])]
    unnamed x79 -> x111, local copies, waits for them, and re-layouts: 4.12 us -> 8.9 us
  transfers between devices with their start and end apart: 7 -> 20, of which waited for: 5 -> 17; matrix products, arithmetic and copies ran while one was open for 12% -> 13% of each run, Pallas kernels for 0% -> 0%
where the time goes in v1:
time: 440 us; the launch traced here: 438 us
  waiting for transfers between devices  166 us (38%)
  blocking collectives  82.6 us (19%)
  other arithmetic  54.4 us (12%)
  local copies, waits for them, and re-layouts  53.6 us (12%)
  between operations  31.3 us (7%)
  matrix products  26.2 us (6%)
  starting transfers between devices  23.8 us (5%)
    ppermute x14, waiting for transfers between devices, body(): lax.ppermute(ring[-1], 'mem', [(dev, (dev + 1) % 8) for dev in range(8)])  138 us
    all_gather x2, blocking collectives, sum_everywhere(): lax.all_gather(jnp.sum(parts, 0), ('mem', 'rep'), axis=0, tiled=True)  82.6 us
    gather x2, local copies, waits for them, and re-layouts, body(): fetched = jnp.take(whole_bf, slot_ids.reshape(-1), axis=0, mode='clip')  24.8 us
    concatenate x2, other arithmetic, body(): jnp.roll(jnp.concatenate(ring[::-1], axis=0), (lax.axis_index('mem') + 1)...  14.9 us
    all_gather x2, waiting for transfers between devices, body(): every_parcel = lax.all_gather(parcel, 'rep', axis=0, tiled=True)  12.8 us
    all_to_all x2, starting transfers between devices, sum_everywhere(): lax.all_to_all(table, ('mem', 'rep'), split_axis=0, concat_axis=0, tiled=...  10.8 us
    all_to_all x2, waiting for transfers between devices, sum_everywhere(): lax.all_to_all(table, ('mem', 'rep'), split_axis=0, concat_axis=0, tiled=...  9.99 us
    unnamed x111, local copies, waits for them, and re-layouts  8.9 us
  transfers between devices with their start and end apart: 20, of which 17 were waited for; matrix products, arithmetic and copies ran while one was open for 13% of the time, Pallas kernels for 0%

profile of v1, /device:TPU:0, one launch (start us, length us, event | category | flops | bytes accessed | tf_op | source)
XLA Modules:
  0.0 438.0 jit_solution(1663895596164415834)
XLA Ops:
  14.6 11.9 %collective-permute-done = bf16[1024,172]{1,0:T(8,128)(2,1)S(1)} collective-permute-done((bf16[1024,172]{1,0:T(8,128)(2,1)S(1)}, bf16[1024,172]{1,0:T(8,128)(2,1)S(1)}, u32[]{:S(2)}, u32[]{:S(2)}) %collective-permute-start) | collective-permute-done | bytes 352288 | tf_op jit(solution)/shard_map/ppermute | solution.py:148
  29.6 12.7 %collective-permute-done.1 = bf16[1024,172]{1,0:T(8,128)(2,1)S(1)} collective-permute-done((bf16[1024,172]{1,0:T(8,128)(2,1)S(1)}, bf16[1024,172]{1,0:T(8,128)(2,1)S(1)}, u32[]{:S(2)}, u32[]{:S(2)}) %collective-permute-start.1) | collective-permute-done | bytes 352288 | tf_op jit(solution)/shard_map/ppermute | solution.py:148
  42.8 14.4 %collective-permute-done.2 = bf16[1024,172]{1,0:T(8,128)(2,1)S(1)} collective-permute-done((bf16[1024,172]{1,0:T(8,128)(2,1)S(1)}, bf16[1024,172]{1,0:T(8,128)(2,1)S(1)}, u32[]{:S(2)}, u32[]{:S(2)}) %collective-permute-start.2) | collective-permute-done | bytes 352288 | tf_op jit(solution)/shard_map/ppermute | solution.py:148
  58.4 12.9 %collective-permute-done.3 = bf16[1024,172]{1,0:T(8,128)(2,1)S(1)} collective-permute-done((bf16[1024,172]{1,0:T(8,128)(2,1)S(1)}, bf16[1024,172]{1,0:T(8,128)(2,1)S(1)}, u32[]{:S(2)}, u32[]{:S(2)}) %collective-permute-start.3) | collective-permute-done | bytes 352288 | tf_op jit(solution)/shard_map/ppermute | solution.py:148
  72.3 12.3 %collective-permute-done.4 = bf16[1024,172]{1,0:T(8,128)(2,1)S(1)} collective-permute-done((bf16[1024,172]{1,0:T(8,128)(2,1)S(1)}, bf16[1024,172]{1,0:T(8,128)(2,1)S(1)}, u32[]{:S(2)}, u32[]{:S(2)}) %collective-permute-start.4) | collective-permute-done | bytes 352288 | tf_op jit(solution)/shard_map/ppermute | solution.py:148
  88.3 8.7 %collective-permute-done.5 = bf16[1024,172]{1,0:T(8,128)(2,1)} collective-permute-done((bf16[1024,172]{1,0:T(8,128)(2,1)S(1)}, bf16[1024,172]{1,0:T(8,128)(2,1)}, u32[]{:S(2)}, u32[]{:S(2)}) %collective-permute-start.5) | collective-permute-done | bytes 352288 | tf_op jit(solution)/shard_map/ppermute | solution.py:148
  100.2 9.0 %collective-permute-done.6 = bf16[1024,172]{1,0:T(8,128)(2,1)} collective-permute-done((bf16[1024,172]{1,0:T(8,128)(2,1)}, bf16[1024,172]{1,0:T(8,128)(2,1)}, u32[]{:S(2)}, u32[]{:S(2)}) %collective-permute-start.6) | collective-permute-done | bytes 352288 | tf_op jit(solution)/shard_map/ppermute | solution.py:148
  111.6 13.4 %fusion.4 = bf16[8192,172]{1,0:T(8,128)(2,1)} fusion(s32[]{:T(128)S(6)} %select_n.172, bf16[8192,172]{1,0:T(8,128)(2,1)S(1)} %constant_dynamic-update-slice_fusion), kind=kLoop, calls=%fused_computation.15 | loop fusion | flops 5636096 | bytes 5636100 | tf_op jit(solution)/shard_map/jit(_roll_dynamic)/concatenate | solution.py:149
  125.0 12.4 %gather_fusion = bf16[4224,172]{1,0:T(8,128)(2,1)S(1)} fusion(bf16[8192,172]{1,0:T(8,128)(2,1)} %fusion.4, s32[5120]{0:T(1024)S(1)} %pad_clamp_fusion.1), kind=kCustom, calls=%fused_computation | custom fusion | bytes 2923008 | tf_op jit(solution)/shard_map/jit(_take)/gather | solution.py:154
  146.4 5.6 %all-to-all-done = bf16[8,64,275]{2,1,0:T(8,128)(2,1)S(1)} async-done(((bf16[8,64,275]{2,1,0:T(8,128)(2,1)}), bf16[8,64,275]{2,1,0:T(8,128)(2,1)S(1)}, u32[]{:S(2)}, u32[]{:S(2)}) %all-to-all-start) | async-done | bytes 281632 | tf_op jit(solution)/shard_map/all_to_all | solution.py:174
  157.6 12.8 %all-gather.3.cloned.1.call-done = bf16[32,64,275]{2,1,0:T(8,128)(2,1)} async-done(((bf16[8,64,275]{2,1,0:T(8,128)(2,1)}), bf16[32,64,275]{2,1,0:T(8,128)(2,1)}) %all-gather.3.cloned.1.call-update) | async-done | bytes 1126416 | tf_op jit(solution)/shard_map/all_gather | solution.py:175
  180.2 10.9 %collective-permute-done.7 = bf16[1024,172]{0,1:T(8,128)(2,1)S(1)} collective-permute-done((bf16[1024,172]{0,1:T(8,128)(2,1)S(1)}, bf16[1024,172]{0,1:T(8,128)(2,1)S(1)}, u32[]{:S(2)}, u32[]{:S(2)}) %collective-permute-start.7) | collective-permute-done | bytes 352288 | tf_op jit(solution)/shard_map/ppermute | solution.py:148
  192.0 11.5 %collective-permute-done.8 = bf16[1024,172]{0,1:T(8,128)(2,1)} collective-permute-done((bf16[1024,172]{0,1:T(8,128)(2,1)S(1)}, bf16[1024,172]{0,1:T(8,128)(2,1)}, u32[]{:S(2)}, u32[]{:S(2)}) %collective-permute-start.8) | collective-permute-done | bytes 352288 | tf_op jit(solution)/shard_map/ppermute | solution.py:148
  208.9 5.1 %all-to-all-start.2 = ((f32[32,24,100]{2,1,0:T(8,128)}), f32[32,24,100]{2,1,0:T(8,128)S(1)}, u32[]{:S(2)}, u32[]{:S(2)}) async-start(f32[32,24,100]{2,1,0:T(8,128)} %bitcast.37), calls=%async_computation.2 | async-start | bytes 786432 | tf_op jit(solution)/shard_map/all_to_all | solution.py:77
  217.4 16.3 %collective-permute-done.10 = bf16[1024,172]{0,1:T(8,128)(2,1)S(1)} collective-permute-done((bf16[1024,172]{0,1:T(8,128)(2,1)S(1)}, bf16[1024,172]{0,1:T(8,128)(2,1)S(1)}, u32[]{:S(2)}, u32[]{:S(2)}) %collective-permute-start.10) | collective-permute-done | bytes 352288 | tf_op jit(solution)/shard_map/ppermute | solution.py:148
  235.0 42.7 %all_gather.14 = f32[768,100]{1,0:T(8,128)S(1)} all-gather(f32[24,100]{1,0:T(8,128)S(1)} %reduce_sum.364), channel_id=1, replica_groups=mesh['mem'=8,'rep'=4] {'mem','rep'}, dimensions={0}, use_global_device_ids=true | all-gather | bytes 316800 | tf_op jit(solution)/shard_map/all_gather | solution.py:78
  286.2 4.9 %collective-permute-done.12 = bf16[1024,172]{0,1:T(8,128)(2,1)S(1)} collective-permute-done((bf16[1024,172]{0,1:T(8,128)(2,1)S(1)}, bf16[1024,172]{0,1:T(8,128)(2,1)S(1)}, u32[]{:S(2)}, u32[]{:S(2)}) %collective-permute-start.12) | collective-permute-done | bytes 352288 | tf_op jit(solution)/shard_map/ppermute | solution.py:148
  292.4 11.2 %collective-permute-done.13 = bf16[1024,172]{0,1:T(8,128)(2,1)S(1)} collective-permute-done((bf16[1024,172]{0,1:T(8,128)(2,1)S(1)}, bf16[1024,172]{0,1:T(8,128)(2,1)S(1)}, u32[]{:S(2)}, u32[]{:S(2)}) %collective-permute-start.13) | collective-permute-done | bytes 352288 | tf_op jit(solution)/shard_map/ppermute | solution.py:148
  306.3 3.9 copy.62
  310.2 12.4 %gather_fusion.1 = bf16[4224,172]{1,0:T(8,128)(2,1)S(1)} fusion(bf16[8192,172]{1,0:T(8,128)(2,1)} %copy.62, s32[5120]{0:T(1024)S(1)} %pad_clamp_fusion), kind=kCustom, calls=%fused_computation.1 | custom fusion | bytes 2923008 | tf_op jit(solution)/shard_map/jit(_take)/gather | solution.py:154
  335.2 4.1 all-to-all-start.1
  350.4 5.7 %all-to-all-start.3 = ((f32[32,24,100]{2,1,0:T(8,128)}), f32[32,24,100]{2,1,0:T(8,128)S(1)}, u32[]{:S(2)}, u32[]{:S(2)}) async-start(f32[32,24,100]{2,1,0:T(8,128)} %bitcast.56), calls=%async_computation.3 | async-start | bytes 786432 | tf_op jit(solution)/shard_map/all_to_all | solution.py:77
  359.8 9.5 %all-to-all-done.3 = f32[32,24,100]{2,1,0:T(8,128)S(1)} async-done(((f32[32,24,100]{2,1,0:T(8,128)}), f32[32,24,100]{2,1,0:T(8,128)S(1)}, u32[]{:S(2)}, u32[]{:S(2)}) %all-to-all-start.3) | async-done | bytes 307232 | tf_op jit(solution)/shard_map/all_to_all | solution.py:77
  369.4 39.9 %all_gather.15 = f32[768,100]{1,0:T(8,128)S(1)} all-gather(f32[24,100]{1,0:T(8,128)S(1)} %reduce_sum.380), channel_id=1, replica_groups=mesh['mem'=8,'rep'=4] {'mem','rep'}, dimensions={0}, use_global_device_ids=true | all-gather | bytes 316800 | tf_op jit(solution)/shard_map/all_gather | solution.py:78
  (250 shorter events, 102.8 us)
Async XLA Ops:
  7.2 90.5 %copy-start = (bf16[172,516]{1,0:T(8,128)(2,1)S(1)}, bf16[172,516]{1,0:T(8,128)(2,1)}, u32[]{:S(2)}) copy-start(bf16[172,516]{1,0:T(8,128)(2,1)} %param.29) | copy-start | bytes 532516
  8.5 18.0 %collective-permute-start = (bf16[1024,172]{1,0:T(8,128)(2,1)S(1)}, bf16[1024,172]{1,0:T(8,128)(2,1)S(1)}, u32[]{:S(2)}, u32[]{:S(2)}) collective-permute-start(bf16[1024,172]{1,0:T(8,128)(2,1)S(1)} %copy.57), channel_id=1, source_target_pairs={{0,4},{4,8},{8,12},{12,16},{16,20},{20,24},{24,28},{28,0},{1,5},{5... | collective-permute-start | bytes 1056776 | tf_op jit(solution)/shard_map/ppermute | solution.py:148
  14.6 56.7 %copy-start.42 = (s32[2,128]{1,0:T(2,128)S(1)}, s32[2,128]{1,0:T(2,128)}, u32[]{:S(2)}) copy-start(s32[2,128]{1,0:T(2,128)} %param.24) | copy-start | bytes 3076
  26.5 15.8 %collective-permute-start.1 = (bf16[1024,172]{1,0:T(8,128)(2,1)S(1)}, bf16[1024,172]{1,0:T(8,128)(2,1)S(1)}, u32[]{:S(2)}, u32[]{:S(2)}) collective-permute-start(bf16[1024,172]{1,0:T(8,128)(2,1)S(1)} %collective-permute-done), channel_id=1, source_target_pairs={{0,4},{4,8},{8,12},{12,16},{16,20},{20,24},{24,28},{28,0},{1,5},{5... | collective-permute-start | bytes 1056776 | tf_op jit(solution)/shard_map/ppermute | solution.py:148
  42.3 14.9 %collective-permute-start.2 = (bf16[1024,172]{1,0:T(8,128)(2,1)S(1)}, bf16[1024,172]{1,0:T(8,128)(2,1)S(1)}, u32[]{:S(2)}, u32[]{:S(2)}) collective-permute-start(bf16[1024,172]{1,0:T(8,128)(2,1)S(1)} %collective-permute-done.1), channel_id=1, source_target_pairs={{0,4},{4,8},{8,12},{12,16},{16,20},{20,24},{24,28},{28,0},{1,5},{5... | collective-permute-start | bytes 1056776 | tf_op jit(solution)/shard_map/ppermute | solution.py:148
  57.2 14.1 %collective-permute-start.3 = (bf16[1024,172]{1,0:T(8,128)(2,1)S(1)}, bf16[1024,172]{1,0:T(8,128)(2,1)S(1)}, u32[]{:S(2)}, u32[]{:S(2)}) collective-permute-start(bf16[1024,172]{1,0:T(8,128)(2,1)S(1)} %collective-permute-done.2), channel_id=1, source_target_pairs={{0,4},{4,8},{8,12},{12,16},{16,20},{20,24},{24,28},{28,0},{1,5},{5... | collective-permute-start | bytes 1056776 | tf_op jit(solution)/shard_map/ppermute | solution.py:148
  71.3 13.2 %collective-permute-start.4 = (bf16[1024,172]{1,0:T(8,128)(2,1)S(1)}, bf16[1024,172]{1,0:T(8,128)(2,1)S(1)}, u32[]{:S(2)}, u32[]{:S(2)}) collective-permute-start(bf16[1024,172]{1,0:T(8,128)(2,1)S(1)} %collective-permute-done.3), channel_id=1, source_target_pairs={{0,4},{4,8},{8,12},{12,16},{16,20},{20,24},{24,28},{28,0},{1,5},{5... | collective-permute-start | bytes 1056776 | tf_op jit(solution)/shard_map/ppermute | solution.py:148
  84.5 12.5 %collective-permute-start.5 = (bf16[1024,172]{1,0:T(8,128)(2,1)S(1)}, bf16[1024,172]{1,0:T(8,128)(2,1)}, u32[]{:S(2)}, u32[]{:S(2)}) collective-permute-start(bf16[1024,172]{1,0:T(8,128)(2,1)S(1)} %collective-permute-done.4), channel_id=1, source_target_pairs={{0,4},{4,8},{8,12},{12,16},{16,20},{20,24},{24,28},{28,0},{1,5},{5... | collective-permute-start | bytes 1056776 | tf_op jit(solution)/shard_map/ppermute | solution.py:148
  97.0 12.2 %collective-permute-start.6 = (bf16[1024,172]{1,0:T(8,128)(2,1)}, bf16[1024,172]{1,0:T(8,128)(2,1)}, u32[]{:S(2)}, u32[]{:S(2)}) collective-permute-start(bf16[1024,172]{1,0:T(8,128)(2,1)} %collective-permute-done.5), channel_id=1, source_target_pairs={{0,4},{4,8},{8,12},{12,16},{16,20},{20,24},{24,28},{28,0},{1,5},{5... | collective-permute-start | bytes 1056776 | tf_op jit(solution)/shard_map/ppermute | solution.py:148
  139.4 12.6 %all-to-all-start = ((bf16[8,64,275]{2,1,0:T(8,128)(2,1)}), bf16[8,64,275]{2,1,0:T(8,128)(2,1)S(1)}, u32[]{:S(2)}, u32[]{:S(2)}) async-start(bf16[8,64,275]{2,1,0:T(8,128)(2,1)} %bitcast.175), calls=%async_computation | async-start | bytes 786432 | tf_op jit(solution)/shard_map/all_to_all | solution.py:174
  142.9 27.5 %all-gather.3.cloned.1.call-start = ((), (), s32[]{:S(2)}) async-start(), calls=%async_computation.4 | async-start | bytes 1966080 | tf_op jit(solution)/shard_map/all_gather | solution.py:175
  177.8 13.2 %collective-permute-start.7 = (bf16[1024,172]{0,1:T(8,128)(2,1)S(1)}, bf16[1024,172]{0,1:T(8,128)(2,1)S(1)}, u32[]{:S(2)}, u32[]{:S(2)}) collective-permute-start(bf16[1024,172]{0,1:T(8,128)(2,1)S(1)} %get-tuple-element.40), channel_id=1, source_target_pairs={{0,4},{4,8},{8,12},{12,16},{16,20},{20,24},{24,28},{28,0},{1,5},{5... | collective-permute-start | bytes 1056776 | tf_op jit(solution)/shard_map/ppermute | solution.py:148
  191.0 12.5 %collective-permute-start.8 = (bf16[1024,172]{0,1:T(8,128)(2,1)S(1)}, bf16[1024,172]{0,1:T(8,128)(2,1)}, u32[]{:S(2)}, u32[]{:S(2)}) collective-permute-start(bf16[1024,172]{0,1:T(8,128)(2,1)S(1)} %collective-permute-done.7), channel_id=1, source_target_pairs={{0,4},{4,8},{8,12},{12,16},{16,20},{20,24},{24,28},{28,0},{1,5},{5... | collective-permute-start | bytes 1056776 | tf_op jit(solution)/shard_map/ppermute | solution.py:148
  203.5 11.7 %collective-permute-start.9 = (bf16[1024,172]{0,1:T(8,128)(2,1)}, bf16[1024,172]{0,1:T(8,128)(2,1)S(1)}, u32[]{:S(2)}, u32[]{:S(2)}) collective-permute-start(bf16[1024,172]{0,1:T(8,128)(2,1)} %collective-permute-done.8), channel_id=1, source_target_pairs={{0,4},{4,8},{8,12},{12,16},{16,20},{20,24},{24,28},{28,0},{1,5},{5... | collective-permute-start | bytes 1056776 | tf_op jit(solution)/shard_map/ppermute | solution.py:148
  208.9 26.1 %all-to-all-start.2 = ((f32[32,24,100]{2,1,0:T(8,128)}), f32[32,24,100]{2,1,0:T(8,128)S(1)}, u32[]{:S(2)}, u32[]{:S(2)}) async-start(f32[32,24,100]{2,1,0:T(8,128)} %bitcast.37), calls=%async_computation.2 | async-start | bytes 786432 | tf_op jit(solution)/shard_map/all_to_all | solution.py:77
  215.2 18.4 %collective-permute-start.10 = (bf16[1024,172]{0,1:T(8,128)(2,1)S(1)}, bf16[1024,172]{0,1:T(8,128)(2,1)S(1)}, u32[]{:S(2)}, u32[]{:S(2)}) collective-permute-start(bf16[1024,172]{0,1:T(8,128)(2,1)S(1)} %collective-permute-done.9), channel_id=1, source_target_pairs={{0,4},{4,8},{8,12},{12,16},{16,20},{20,24},{24,28},{28,0},{1,5},{5... | collective-permute-start | bytes 1056776 | tf_op jit(solution)/shard_map/ppermute | solution.py:148
  233.7 44.0 %collective-permute-start.11 = (bf16[1024,172]{0,1:T(8,128)(2,1)S(1)}, bf16[1024,172]{0,1:T(8,128)(2,1)S(1)}, u32[]{:S(2)}, u32[]{:S(2)}) collective-permute-start(bf16[1024,172]{0,1:T(8,128)(2,1)S(1)} %collective-permute-done.10), channel_id=1, source_target_pairs={{0,4},{4,8},{8,12},{12,16},{16,20},{20,24},{24,28},{28,0},{1,5},{5... | collective-permute-start | bytes 1056776 | tf_op jit(solution)/shard_map/ppermute | solution.py:148
  234.5 70.2 %copy-start.21 = (bf16[1024,172]{0,1:T(8,128)(2,1)S(1)}, bf16[1024,172]{0,1:T(8,128)(2,1)}, u32[]{:S(2)}) copy-start(bf16[1024,172]{0,1:T(8,128)(2,1)} %copy-done.20) | copy-start | bytes 1056772
  277.7 13.4 %collective-permute-start.12 = (bf16[1024,172]{0,1:T(8,128)(2,1)S(1)}, bf16[1024,172]{0,1:T(8,128)(2,1)S(1)}, u32[]{:S(2)}, u32[]{:S(2)}) collective-permute-start(bf16[1024,172]{0,1:T(8,128)(2,1)S(1)} %collective-permute-done.11), channel_id=1, source_target_pairs={{0,4},{4,8},{8,12},{12,16},{16,20},{20,24},{24,28},{28,0},{1,5},{5... | collective-permute-start | bytes 1056776 | tf_op jit(solution)/shard_map/ppermute | solution.py:148
  291.1 12.5 %collective-permute-start.13 = (bf16[1024,172]{0,1:T(8,128)(2,1)S(1)}, bf16[1024,172]{0,1:T(8,128)(2,1)S(1)}, u32[]{:S(2)}, u32[]{:S(2)}) collective-permute-start(bf16[1024,172]{0,1:T(8,128)(2,1)S(1)} %collective-permute-done.12), channel_id=1, source_target_pairs={{0,4},{4,8},{8,12},{12,16},{16,20},{20,24},{24,28},{28,0},{1,5},{5... | collective-permute-start | bytes 1056776 | tf_op jit(solution)/shard_map/ppermute | solution.py:148
  335.2 15.2 %all-to-all-start.1 = ((bf16[8,64,275]{2,1,0:T(8,128)(2,1)}), bf16[8,64,275]{2,1,0:T(8,128)(2,1)}, u32[]{:S(2)}, u32[]{:S(2)}) async-start(bf16[8,64,275]{2,1,0:T(8,128)(2,1)} %bitcast.174), calls=%async_computation.1 | async-start | bytes 786432 | tf_op jit(solution)/shard_map/all_to_all | solution.py:174
  350.4 19.0 %all-to-all-start.3 = ((f32[32,24,100]{2,1,0:T(8,128)}), f32[32,24,100]{2,1,0:T(8,128)S(1)}, u32[]{:S(2)}, u32[]{:S(2)}) async-start(f32[32,24,100]{2,1,0:T(8,128)} %bitcast.56), calls=%async_computation.3 | async-start | bytes 786432 | tf_op jit(solution)/shard_map/all_to_all | solution.py:77
  356.1 67.2 %all-gather.5.cloned.1.call-start = ((), (), s32[]{:S(2)}) async-start(), calls=%async_computation.5 | async-start | bytes 1966080 | tf_op jit(solution)/shard_map/all_gather | solution.py:175
  357.5 62.1 %copy-start.39 = (f32[100]{0:T(128)S(1)}, f32[100]{0:T(128)}, u32[]{:S(2)}) copy-start(f32[100]{0:T(128)} %copy-done.38) | copy-start | bytes 1204
  (44 other events, 365.0 us)
Sparse Core Ops, SparseCore 0:
  152.9 17.4 all-gather.2
  359.4 21.7 all-gather.4
